TPU v7x, 256 devices: a whole 4x4x8 slice. The times are simulated.
256 devices in a mesh: grp: 16 (over y_hi, x, core), shard: 16 (over z, y_lo).
Axes of the slice: x: 4, y: 4 (y_hi: 2, y_lo: 2; y = y_hi * 2 + y_lo), z: 8, core: 2. Of those that a mesh axis runs over, the one named last changes fastest.
Arguments:
- gradients: bfloat16 [16, 1024, 5120], P('grp', None, 'shard'), may hold values from -150 to 150
- left_factor: bfloat16 [16, 1024, 1024], P('grp'), may hold values from -1 to 2, as said below
- right_factor: bfloat16 [16, 5120, 5120], P('grp', 'shard'), may hold values from -1 to 2, as said below
Outputs:
- update: bfloat16 [16, 1024, 5120], P('grp', None, 'shard')
Inputs may be any that keep to these rules, and one draw needn't show every extreme that they name: `left_factor`: each factor is upper triangular with a positive diagonal. `right_factor`: each factor is upper triangular with a positive diagonal.
All inputs are finite; a program needn't handle non-finite values.
Results may differ from a plain program's by a relative error of at most 0.0061.
Values may be sent and summed in bfloat16 or wider, within the bound.
A program may use at most 128 MiB of HBM per device.

v0:
```python
import functools

import jax
import jax.numpy as jnp
from jax import lax
from jax.sharding import Mesh
from jax.sharding import PartitionSpec as P

SHARD = ("shard_0", "shard_1")
GRP_SHARD = ("grp_0", "grp_1", "grp_2", "shard_0", "shard_1")
GRP = ("grp_0", "grp_1", "grp_2")


def gathered_by_axis(value, axes, dim):
    for axis in reversed(axes):
        value = lax.all_gather(value, axis, axis=dim, tiled=True)
    return value


def summed_rows(subtotal, axes):
    for axis in axes:
        subtotal = lax.psum_scatter(subtotal, axis, scatter_dimension=0, tiled=True)
    return subtotal


def over_axes(value, axes):
    return functools.reduce(lax.psum, axes, value)


def body(gradients, left_factor, right_factor):
    squares = jnp.float32(0.0)
    gradient = gradients[0]
    left_q = left_factor[0]
    right_rows = right_factor[0]
    block = right_rows
    first = lax.dot_general(
        gathered_by_axis(gradient, SHARD, 1),
        block,
        (((1,), (1,)), ((), ())),
        preferred_element_type=jnp.float32,
    ).astype(jnp.bfloat16)
    block = right_rows
    second_rows = summed_rows(
        lax.dot_general(block, first, (((0,), (1,)), ((), ())), preferred_element_type=jnp.float32),
        SHARD,
    ).astype(jnp.bfloat16)
    second = second_rows.T
    third = jnp.dot(left_q, second, preferred_element_type=jnp.float32).astype(jnp.bfloat16)
    precond = lax.dot_general(
        left_q, third, (((0,), (0,)), ((), ())), preferred_element_type=jnp.float32
    )
    results = [precond]
    squares = jnp.sum(precond * precond)
    total = over_axes(squares, GRP_SHARD)
    count = (
        gradients.shape[0]
        * lax.axis_size(GRP)
        * gradients.shape[1]
        * gradients.shape[2]
        * lax.axis_size(SHARD)
    )
    rms = jnp.sqrt(total / count + 1e-06)
    factor = jnp.minimum(jnp.float32(1.0), 1.1 / rms)
    stacked = jnp.stack(results, axis=0)
    return (stacked * factor).astype(jnp.bfloat16)


def solution(mesh):
    split = Mesh(
        mesh.devices.reshape(2, 4, 2, 8, 2), ("grp_0", "grp_1", "grp_2", "shard_0", "shard_1")
    )
    in_specs = (P(GRP, None, SHARD), P(GRP, None, None), P(GRP, SHARD, None))
    out_specs = P(GRP, None, SHARD)
    return jax.shard_map(body, mesh=split, in_specs=in_specs, out_specs=out_specs, check_vma=False)
```

profile of v0, /device:TPU:1, one launch (start us, length us, event | category | flops | bytes accessed | tf_op | source)
XLA Modules:
  0.0 491.4 jit_solution(13046331759293419991)
XLA Ops:
  6.5 0.0 copy-start
  6.5 0.0 all-gather.5.cloned.1.call-start
  6.5 0.7 all-gather.5.cloned.1.call-update
  7.3 0.0 all-gather.7.cloned.1.call-start
  7.3 34.8 %all-gather.5.cloned.1.call-done = bf16[1,1024,640]{1,2,0:T(8,128)(2,1)} async-done(((bf16[1,1024,320]{1,2,0:T(8,128)(2,1)}), bf16[1,1024,640]{1,2,0:T(8,128)(2,1)}) %all-gather.5.cloned.1.call-update) | async-done | bytes 1310736 | tf_op jit(solution)/shard_map/all_gather | solution.py:16
  42.1 0.0 all-gather.7.cloned.1.call-update
  42.1 0.0 reduce-scatter.5.cloned.1.call-start
  42.2 116.5 %all-gather.7.cloned.1.call-done = bf16[1,1024,5120]{1,2,0:T(8,128)(2,1)} async-done(((bf16[1,1024,640]{1,2,0:T(8,128)(2,1)}), bf16[1,1024,5120]{1,2,0:T(8,128)(2,1)}) %all-gather.7.cloned.1.call-update) | async-done | bytes 10485776 | tf_op jit(solution)/shard_map/all_gather | solution.py:16
  158.7 0.0 copy-done
  158.7 17.6 %convolution_bitcast_fusion = f32[5120,1024]{0,1:T(8,128)} fusion(bf16[1,320,5120]{2,1,0:T(8,128)(2,1)S(1)} %copy-done, bf16[1,1024,5120]{1,2,0:T(8,128)(2,1)} %all-gather.7.cloned.1.call-done), kind=kOutput, calls=%fused_computation | convolution fusion | flops 6711214080 | bytes 34734080 | tf_op jit(solution)/shard_map/dot_general | solution.py:44
  176.3 0.0 reduce-scatter.5.cloned.1.call-update
  176.3 0.0 reduce-scatter.7.cloned.1.call-start
  176.3 211.8 %reduce-scatter.5.cloned.1.call-done = f32[640,1024]{0,1:T(8,128)} async-done(((f32[5120,1024]{0,1:T(8,128)}), f32[640,1024]{0,1:T(8,128)}) %reduce-scatter.5.cloned.1.call-update) | async-done | bytes 2621456 | tf_op jit(solution)/shard_map/reduce_scatter | solution.py:22
  388.2 3.2 copy.4
  391.4 0.0 reduce-scatter.7.cloned.1.call-update
  391.4 41.4 %reduce-scatter.7.cloned.1.call-done = f32[320,1024]{1,0:T(8,128)} async-done(((f32[640,1024]{1,0:T(8,128)}), f32[320,1024]{1,0:T(8,128)}) %reduce-scatter.7.cloned.1.call-update) | async-done | bytes 1310736
  432.9 2.5 copy.5
  435.4 5.9 %multiply_reduce_fusion = (f32[]{:T(128)}, f32[320,1024]{1,0:T(8,128)}) fusion(bf16[1,1024,1024]{2,1,0:T(8,128)(2,1)} %param.4, bf16[320,1024]{0,1:T(8,128)(2,1)} %copy.5), kind=kOutput, calls=%fused_computation.12 | convolution fusion | flops 1343160320 | bytes 4063236 | tf_op jit(solution)/shard_map/dot_general | solution.py:49
  441.3 5.9 %psum.35 = f32[]{:T(128)} all-reduce(f32[]{:T(128)} %get-tuple-element.5), channel_id=1, replica_groups=mesh['grp_0'=2,'grp_1'=4,'grp_2'=2,'shard_0'=8,'shard_1'=2] {'grp_0'}, use_global_device_ids=true, to_apply=%region_3.0 | all-reduce | flops 1 | bytes 8 | tf_op jit(solution)/shard_map/psum | solution.py:27
  447.2 9.0 %psum.36 = f32[]{:T(128)} all-reduce(f32[]{:T(128)} %psum.35), channel_id=1, replica_groups=mesh['grp_0'=2,'grp_1'=4,'grp_2'=2,'shard_0'=8,'shard_1'=2] {'grp_1'}, use_global_device_ids=true, to_apply=%region_4.0 | all-reduce | flops 1 | bytes 8 | tf_op jit(solution)/shard_map/psum | solution.py:27
  456.2 6.7 %psum.37 = f32[]{:T(128)} all-reduce(f32[]{:T(128)} %psum.36), channel_id=1, replica_groups=mesh['grp_0'=2,'grp_1'=4,'grp_2'=2,'shard_0'=8,'shard_1'=2] {'grp_2'}, use_global_device_ids=true, to_apply=%region_5.0 | all-reduce | flops 1 | bytes 8 | tf_op jit(solution)/shard_map/psum | solution.py:27
  462.9 14.6 %psum.38 = f32[]{:T(128)} all-reduce(f32[]{:T(128)} %psum.37), channel_id=1, replica_groups=mesh['grp_0'=2,'grp_1'=4,'grp_2'=2,'shard_0'=8,'shard_1'=2] {'shard_0'}, use_global_device_ids=true, to_apply=%region_6.0 | all-reduce | flops 1 | bytes 8 | tf_op jit(solution)/shard_map/psum | solution.py:27
  477.6 4.4 psum.39
  482.6 2.3 fusion.24
Async XLA Ops:
  6.5 152.1 %copy-start = (bf16[1,320,5120]{2,1,0:T(8,128)(2,1)S(1)}, bf16[1,320,5120]{2,1,0:T(8,128)(2,1)}, u32[]{:S(2)}) copy-start(bf16[1,320,5120]{2,1,0:T(8,128)(2,1)} %param.5) | copy-start | bytes 9830404
  6.5 35.6 %all-gather.5.cloned.1.call-start = ((), (), s32[]{:S(2)}) async-start(), calls=%async_computation.3 | async-start | bytes 1966080 | tf_op jit(solution)/shard_map/all_gather | solution.py:16
  7.3 151.4 %all-gather.7.cloned.1.call-start = ((), (), s32[]{:S(2)}) async-start(), calls=%async_computation.4 | async-start | bytes 11796480 | tf_op jit(solution)/shard_map/all_gather | solution.py:16
  42.1 346.1 %reduce-scatter.5.cloned.1.call-start = ((), (), s32[]{:S(2)}) async-start(), calls=%async_computation.2 | async-start | bytes 23592960 | tf_op jit(solution)/shard_map/reduce_scatter | solution.py:22
  176.3 256.6 %reduce-scatter.7.cloned.1.call-start = ((), (), s32[]{:S(2)}) async-start(), calls=%async_computation.5 | async-start | bytes 3932160
Sparse Core Ops, SparseCore 0:
  9.1 32.9 all-gather.4
  43.9 114.7 all-gather.6
  176.4 211.7 reduce-scatter.4
  391.5 41.2 reduce-scatter.6
where the time goes:
time: 495 us; the launch traced here: 491 us
  waiting for transfers between devices  405 us (82%)
  blocking collectives  40.6 us (8%)
  matrix products  23.5 us (5%)
  between operations  13.8 us (3%)
  local copies, waits for them, and re-layouts  5.75 us (1%)
    reduce_scatter x1, waiting for transfers between devices, summed_rows(): subtotal = lax.psum_scatter(subtotal, axis, scatter_dimension=0, tiled=True)  212 us
    all_gather x2, waiting for transfers between devices, gathered_by_axis(): value = lax.all_gather(value, axis, axis=dim, tiled=True)  151 us
    unnamed x5, waiting for transfers between devices  42.2 us
    psum x5, blocking collectives, over_axes(): return functools.reduce(lax.psum, axes, value)  40.6 us
    dot_general x1, matrix products, body(): lax.dot_general(block, first, (((0,), (1,)), ((), ())), preferred_element...  17.6 us
  transfers between devices with their start and end apart: 4, of which 4 were waited for; matrix products, arithmetic and copies ran while one was open for 0% of the time, Pallas kernels for 0%

commit v1 on v0

v1 whole, which is shorter than its diff:
```python
import functools

import jax
import jax.numpy as jnp
from jax import lax
from jax.experimental import pallas as pl
from jax.experimental.pallas import tpu as pltpu
from jax.sharding import Mesh
from jax.sharding import PartitionSpec as P

MESH = pl.DeviceIdType.MESH
SHARD = ("shard_0", "shard_1")
GRP = ("grp_0", "grp_1", "grp_2")
F32 = jnp.float32
BF16 = jnp.bfloat16

PLANES = 8
LANES = 128
HOPS = 4


def low(s):
    return jnp.where(s >= 4, 1, 0) + jnp.where(s >= 5, 1, 0) + jnp.where(s >= 7, 1, 0)


def single(s):
    return (s == 3) | (s >= 5)


def loop(lower, upper, body):
    def step(i, carry):
        body(i)
        return carry

    lax.fori_loop(lower, upper, step, 0)


def kernel(
    count,
    sizes,
    g_ref,
    qr_hbm,
    ql_hbm,
    out_ref,
    gt,
    buf,
    yin,
    qr,
    qrt,
    ql,
    first,
    second,
    precond,
    mine,
    all_shard,
    all_grp,
    down_send,
    up_send,
    cross_send,
    back_send,
    rcross_send,
    gz_recv,
    gy_recv,
    rz_recv,
    ry_recv,
    load_sem,
    ar_send,
    ar_recv,
):
    planes, chunks = PLANES, gt.shape[0]
    nb = g_ref.shape[1]
    z, y = lax.axis_index("shard_0"), lax.axis_index("shard_1")
    g0, g1, g2 = lax.axis_index("grp_0"), lax.axis_index("grp_1"), lax.axis_index("grp_2")
    n1, n2 = sizes[1], sizes[2]
    n_shard, n_grp = planes * 2, sizes[0] * n1 * n2
    shard_me = z * 2 + y
    grp_me = (g0 * n1 + g1) * n2 + g2
    up_z, down_z = lax.rem(z + 1, planes), lax.rem(z + planes - 1, planes)
    own = pl.ds(pl.multiple_of(y * nb, 16), nb)
    other = pl.ds(pl.multiple_of((1 - y) * nb, 16), nb)

    def shard_id(p):
        return {"shard_0": p // 2, "shard_1": lax.rem(p, 2)}

    def grp_id(p):
        return {"grp_0": p // (n1 * n2), "grp_1": lax.rem(p // n2, n1), "grp_2": lax.rem(p, n2)}

    def load(s):
        columns = pl.ds(pl.multiple_of(s * 2 * nb, 128), 2 * nb)
        return pltpu.make_async_copy(qr_hbm.at[:, columns], qr.at[s], load_sem.at[s])

    load_ql = pltpu.make_async_copy(ql_hbm, ql, load_sem.at[planes])
    loop(z, planes, lambda s: load(s).start())
    load_ql.start()

    barrier = pltpu.get_barrier_semaphore()

    def greet_shard(k):
        peer = lax.rem(shard_me + k, n_shard)
        pl.semaphore_signal(barrier, inc=1, device_id=shard_id(peer), device_id_type=MESH)

    def greet_grp(k):
        peer = lax.rem(grp_me + k, n_grp)
        pl.semaphore_signal(barrier, inc=1, device_id=grp_id(peer), device_id_type=MESH)

    loop(1, n_shard, greet_shard)
    loop(1, n_grp, greet_grp)

    def place(c):
        rows = pl.ds(pl.multiple_of(c * LANES, LANES), LANES)
        gt[c, z, own, :] = g_ref[rows, :].T

    loop(0, chunks, place)
    pl.semaphore_wait(barrier, n_shard + n_grp - 2)

    def remote(src, dst, send, recv, to_z, to_y):
        return pltpu.make_async_remote_copy(
            src_ref=src,
            dst_ref=dst,
            send_sem=send,
            recv_sem=recv,
            device_id={"shard_0": to_z, "shard_1": to_y},
            device_id_type=MESH,
        )

    def sized(s, act):
        pl.when(single(s))(lambda: act(own))
        pl.when(jnp.logical_not(single(s)))(lambda: act(pl.ds(0, 2 * nb)))

    def down(c, s, rows):
        ref = gt.at[c, s, rows]
        return remote(ref, ref, down_send.at[lax.rem(c, 2), s], gz_recv.at[c, s], down_z, y)

    def up(c, s, rows):
        ref = gt.at[c, s, rows]
        return remote(ref, ref, up_send.at[lax.rem(c, 2), s], gz_recv.at[c, s], up_z, y)

    def cross(c, s):
        ref = gt.at[c, s, own]
        return remote(ref, ref, cross_send.at[lax.rem(c, 2), s], gy_recv.at[c, s], z, 1 - y)

    def back(c, s, rows):
        rising = (z < s) & (z >= low(s))
        parent = jnp.where(rising, up_z, down_z)
        slot = jnp.where((parent == s) & jnp.logical_not(rising), planes, s)
        src = buf.at[jnp.where(z > s, 1, 0), c, s, rows]
        dst = buf.at[1, c, slot, rows]
        return remote(src, dst, back_send.at[lax.rem(c, 2), s], rz_recv.at[c, slot], parent, y)

    def rcross(c, s):
        return remote(
            buf.at[0, c, s, other], yin.at[c, s], rcross_send.at[lax.rem(c, 2), s], ry_recv.at[c, s], z, 1 - y
        )

    def goes_down(s):
        return (z <= s) & (z - 1 >= low(s))

    def goes_up(s):
        return ((z >= s) & (low(s) > 0)) | ((z < s) & (z + 1 < low(s)))

    def crosses(s):
        return (s == z) | ((s > z) & single(s))

    def goes_back(s):
        return (z < s) | ((z > s) & (low(s) > 0))

    def start(c, make):
        pl.when(c >= 2)(lambda: make(c - 2).wait_send())
        make(c).start()

    def start_sized(c, s, make):
        sized(s, lambda rows: start(c, lambda k: make(k, s, rows)))

    def got_gather(c, s):
        sized(s, lambda rows: down(c, s, rows).wait_recv())

    def got_back(c, slot, rows):
        ref = buf.at[1, c, slot, rows]
        remote(ref, ref, back_send.at[0, 0], rz_recv.at[c, slot], up_z, y).wait_recv()

    def valid(c):
        return (c >= 0) & (c < chunks)

    def gather_own(i):
        pl.when(valid(i))(lambda: start(i, lambda k: cross(k, z)))

        c = i - 1

        @pl.when(valid(c))
        def _():
            cross(c, z).wait_recv()
            pl.when(goes_down(z))(lambda: start_sized(c, z, down))
            pl.when(goes_up(z))(lambda: start_sized(c, z, up))

    def gather_hop(i, h):
        c = i - 1 - h
        s = z + h

        @pl.when(valid(c) & (s < planes) & (z >= low(s)))
        def _():
            got_gather(c, s)
            pl.when(goes_down(s))(lambda: start_sized(c, s, down))
            pl.when(single(s))(lambda: start(c, lambda k: cross(k, s)))

        t = lax.rem(z - h + planes, planes)

        @pl.when(valid(c) & (((z > t) & (low(t) > 0)) | ((z < t) & (z < low(t)))))
        def _():
            got_gather(c, t)
            pl.when(goes_up(t))(lambda: start_sized(c, t, up))
            pl.when((z < t) & single(t))(lambda: start(c, lambda k: cross(k, t)))

    def compute(i):
        c = i - 2 - HOPS

        @pl.when(valid(c))
        def _():
            def arrived(s):
                pl.when(single(s))(lambda: cross(c, s).wait_recv())

            loop(z + 1, planes, arrived)

            def gathered(s, total):
                return total + jnp.dot(qr[s], gt[c, s], preferred_element_type=F32)

            total = lax.fori_loop(z, planes, gathered, jnp.zeros((nb, LANES), F32))
            first[c] = total.astype(BF16)

            def share(s):
                buf[0, c, s] = jnp.dot(qrt[s], first[c], preferred_element_type=F32).astype(BF16)
                pl.when((s > z) & single(s))(lambda: start(c, lambda k: rcross(k, s)))

            loop(z, planes, share)

    def back_hop(i, h):
        c = i - 3 - HOPS - (HOPS - h)

        def contribute(s, child):
            @pl.when(single(s))
            def _():
                rcross(c, s).wait_recv()
                pl.when(child)(lambda: got_back(c, s, own))
                pl.when(child)(lambda: add(s, True))
                pl.when(jnp.logical_not(child))(lambda: add(s, False))

            @pl.when(jnp.logical_not(single(s)) & child)
            def _():
                got_back(c, s, pl.ds(0, 2 * nb))
                buf[0, c, s] = (buf[0, c, s].astype(F32) + buf[1, c, s].astype(F32)).astype(BF16)

            start_sized(c, s, back)

        def add(s, child):
            value = buf[0, c, s, own, :].astype(F32) + yin[c, s].astype(F32)
            if child:
                value = value + buf[1, c, s, own, :].astype(F32)
            buf[0, c, s, own, :] = value.astype(BF16)

        s = z + h

        @pl.when(valid(c) & (s < planes) & (z >= low(s)))
        def _():
            contribute(s, z - 1 >= low(s))

        t = lax.rem(z - h + planes, planes)

        @pl.when(valid(c) & (z < t) & (z < low(t)))
        def _():
            contribute(t, z + 1 < low(t))

        @pl.when(valid(c) & (z > t) & (low(t) > 0))
        def _():
            sized(t, lambda rows: got_back(c, t, rows))
            start_sized(c, t, back)

    def root(i):
        c = i - 3 - 2 * HOPS

        @pl.when(valid(c))
        def _():
            pl.when(z > 0)(lambda: sized(z, lambda rows: got_back(c, z, rows)))
            pl.when(low(z) > 0)(lambda: sized(z, lambda rows: got_back(c, planes, rows)))

            @pl.when((z > 0) & jnp.logical_not(single(z)))
            def _():
                buf[0, c, z, other, :] = (
                    buf[0, c, z, other, :].astype(F32) + buf[1, c, z, other, :].astype(F32)
                ).astype(BF16)

                @pl.when(low(z) > 0)
                def _():
                    buf[0, c, z, other, :] = (
                        buf[0, c, z, other, :].astype(F32) + buf[1, c, planes, other, :].astype(F32)
                    ).astype(BF16)

            start(c, lambda k: rcross(k, z))

        d = c - 1

        @pl.when(valid(d))
        def _():
            rcross(d, z).wait_recv()
            total = jnp.dot(qrt[z, own, :], first[d], preferred_element_type=F32) + yin[d, z].astype(F32)
            precond[:, :LANES] = total
            pl.when(z > 0)(lambda: gain(d, z))
            pl.when(low(z) > 0)(lambda: gain(d, planes))
            second[d] = precond[:, :LANES].astype(BF16)

    def gain(d, slot):
        precond[:, :LANES] += buf[1, d, slot, own, :].astype(F32)

    def turn(s):
        load(s).wait()
        qrt[s] = qr[s].T

    def step(i):
        gather_own(i)
        loop(1, HOPS + 1, lambda h: gather_hop(i, h))
        pl.when((2 * i < planes) & (2 * i >= z))(lambda: turn(2 * i))
        pl.when((2 * i + 1 < planes) & (2 * i + 1 >= z))(lambda: turn(2 * i + 1))
        compute(i)
        loop(1, HOPS + 1, lambda h: back_hop(i, h))
        root(i)

    loop(0, chunks + 4 + 2 * HOPS, step)

    load_ql.wait()
    sub = jnp.concatenate([second[c] for c in range(chunks)], axis=1)
    third = lax.dot_general(sub, ql[...], (((1,), (1,)), ((), ())), preferred_element_type=F32).astype(BF16)
    precond[...] = jnp.dot(third, ql[...], preferred_element_type=F32)

    value = precond[...]
    square = value * value
    tile = square[0:8]
    for r in range(8, nb, 8):
        tile = tile + square[r : r + 8]
    total = tile[:, 0:128]
    for k in range(128, value.shape[1], 128):
        total = total + tile[:, k : k + 128]
    mine[...] = total

    def exchange(phase, n, me, ident, slots):
        slots[me] = mine[...]

        def make(peer, at):
            return pltpu.make_async_remote_copy(
                src_ref=mine,
                dst_ref=slots.at[at],
                send_sem=ar_send.at[phase, peer],
                recv_sem=ar_recv.at[phase, at],
                device_id=ident(peer),
                device_id_type=MESH,
            )

        loop(1, n, lambda k: make(lax.rem(me + k, n), me).start())

        def wait(k):
            peer = lax.rem(me + k, n)
            make(peer, peer).wait_recv()

        loop(1, n, wait)
        loop(1, n, lambda k: make(lax.rem(me + k, n), me).wait_send())
        total = slots[0]
        for k in range(1, n):
            total = total + slots[k]
        mine[...] = total

    exchange(0, n_shard, shard_me, shard_id, all_shard)
    exchange(1, n_grp, grp_me, grp_id, all_grp)

    rms = jnp.sqrt(jnp.sum(mine[...], keepdims=True) / count + 1e-06)
    factor = jnp.minimum(jnp.float32(1.0), 1.1 / rms)
    out_ref[...] = (precond[...] * factor).astype(BF16)

    def drain(s):
        for c in range(chunks - 2, chunks):
            pl.when(goes_down(s))(lambda: sized(s, lambda rows: down(c, s, rows).wait_send()))
            pl.when(goes_up(s))(lambda: sized(s, lambda rows: up(c, s, rows).wait_send()))
            pl.when(crosses(s))(lambda: cross(c, s).wait_send())
            pl.when(goes_back(s))(lambda: sized(s, lambda rows: back(c, s, rows).wait_send()))
            pl.when(crosses(s))(lambda: rcross(c, s).wait_send())

    loop(0, planes, drain)


def body(sizes, gradients, left_factor, right_factor):
    rows, nb = gradients.shape[1:]
    chunks = rows // LANES
    planes = PLANES
    n_shard, n_grp = 2 * planes, sizes[0] * sizes[1] * sizes[2]
    count = gradients.shape[0] * n_grp * rows * nb * n_shard
    dma = pltpu.SemaphoreType.DMA
    turned = pl.pallas_call(
        functools.partial(kernel, count, sizes),
        out_shape=jax.ShapeDtypeStruct((nb, rows), BF16),
        in_specs=[
            pl.BlockSpec(memory_space=pltpu.VMEM),
            pl.BlockSpec(memory_space=pl.ANY),
            pl.BlockSpec(memory_space=pl.ANY),
        ],
        out_specs=pl.BlockSpec(memory_space=pltpu.VMEM),
        scratch_shapes=[
            pltpu.VMEM((chunks, planes, 2 * nb, LANES), BF16),
            pltpu.VMEM((2, chunks, planes + 1, 2 * nb, LANES), BF16),
            pltpu.VMEM((chunks, planes, nb, LANES), BF16),
            pltpu.VMEM((planes, nb, 2 * nb), BF16),
            pltpu.VMEM((planes, 2 * nb, nb), BF16),
            pltpu.VMEM((rows, rows), BF16),
            pltpu.VMEM((chunks, nb, LANES), BF16),
            pltpu.VMEM((chunks, nb, LANES), BF16),
            pltpu.VMEM((nb, rows), F32),
            pltpu.VMEM((8, 128), F32),
            pltpu.VMEM((n_shard, 8, 128), F32),
            pltpu.VMEM((n_grp, 8, 128), F32),
            dma((2, planes)),
            dma((2, planes)),
            dma((2, planes)),
            dma((2, planes)),
            dma((2, planes)),
            dma((chunks, planes)),
            dma((chunks, planes)),
            dma((chunks, planes + 1)),
            dma((chunks, planes)),
            dma((planes + 1,)),
            dma((2, max(n_shard, n_grp))),
            dma((2, max(n_shard, n_grp))),
        ],
        compiler_params=pltpu.CompilerParams(
            collective_id=0, has_side_effects=True, vmem_limit_bytes=67043328
        ),
        name="precondition",
    )(gradients[0], right_factor[0], left_factor[0])
    return turned.T[None]


def split_mesh(devices, sizes):
    return Mesh(devices.reshape(*sizes, PLANES, 2), GRP + SHARD)


def program(split, sizes):
    in_specs = (P(GRP, None, SHARD), P(GRP, None, None), P(GRP, SHARD, None))
    return jax.shard_map(
        functools.partial(body, sizes), mesh=split, in_specs=in_specs, out_specs=P(GRP, None, SHARD), check_vma=False
    )


def solution(mesh):
    sizes = (2, 4, 2)
    return program(split_mesh(mesh.devices, sizes), sizes)
```

time: 495 us -> 205 us (0.41)
  waiting for transfers between devices: 405 us -> 0 us
  Pallas kernels: 0 us -> 200 us
  blocking collectives: 40.6 us -> 0 us
  matrix products: 23.5 us -> 0 us
  between operations: 13.8 us -> 0.01 us
    reduce_scatter x1 -> x0, waiting for transfers between devices: 212 us -> none  [summed_rows(): subtotal = lax.psum_scatter(subtotal, axis, scatter_dimension=0, tiled=True)]
    pallas_call x0 -> x1, Pallas kernels: none -> 200 us  [body(): pl.pallas_call(functools.partial(kernel, count, sizes), out_shape=jax.Sha...]
    all_gather x2 -> x0, waiting for transfers between devices: 151 us -> none  [gathered_by_axis(): value = lax.all_gather(value, axis, axis=dim, tiled=True)]
    unnamed x5 -> x0, waiting for transfers between devices: 42.2 us -> none
    psum x5 -> x0, blocking collectives: 40.6 us -> none  [over_axes(): return functools.reduce(lax.psum, axes, value)]
    dot_general x2 -> x0, matrix products: 23.5 us -> none  [the longest x1 17.6 us: body(): lax.dot_general(block, first, (((0,), (1,)), ((), ())), preferred_element...]
  transfers between devices with their start and end apart: 4 -> 0, of which waited for: 4 -> 0; matrix products, arithmetic and copies ran while one was open for 0% -> 0% of each run, Pallas kernels for 0% -> 0%
where the time goes in v1:
time: 205 us; the launch traced here: 204 us
  Pallas kernels  200 us (98%)
  local copies, waits for them, and re-layouts  4.2 us (2%)
    pallas_call x1, Pallas kernels, body(): pl.pallas_call(functools.partial(kernel, count, sizes), out_shape=jax.Sha...  200 us
    unnamed x2, local copies, waits for them, and re-layouts  4.2 us

profile of v1, /device:TPU:1, one launch (start us, length us, event | category | flops | bytes accessed | tf_op | source)
XLA Modules:
  0.0 204.3 jit_solution(2438860248818214811)
XLA Ops:
  0.0 2.2 %copy.4 = bf16[1,1024,320]{2,1,0:T(8,128)(2,1)} copy(bf16[1,1024,320]{1,2,0:T(8,128)(2,1)} %param.3) | data formatting | bytes 1310720 | tf_op args[0]
  2.2 200.1 %precondition.1 = bf16[320,1024]{1,0:T(8,128)(2,1)} custom-call(bf16[1024,320]{1,0:T(8,128)(2,1)} %bitcast.7, bf16[320,5120]{1,0:T(8,128)(2,1)} %bitcast.6, bf16[1024,1024]{1,0:T(8,128)(2,1)} %bitcast.9), custom_call_target="tpu_custom_call" | custom-call | tf_op jit(solution)/shard_map/precondition/pallas_call | solution.py:393
  202.4 2.0 copy.6

commit v2 on v1

v2 whole, which is shorter than its diff:
```python
import functools

import jax
import jax.numpy as jnp
from jax import lax
from jax.experimental import pallas as pl
from jax.experimental.pallas import tpu as pltpu
from jax.sharding import Mesh
from jax.sharding import PartitionSpec as P

MESH = pl.DeviceIdType.MESH
SHARD = ("shard_0", "shard_1")
GRP = ("grp_0", "grp_1", "grp_2")
F32 = jnp.float32
BF16 = jnp.bfloat16

PLANES = 8
LANES = 128
HOPS = 4


def low(s, c, chunks):
    return jnp.where(s >= 5, s - 3, jnp.where((s == 4) & (c >= chunks // 2), 1, 0))


def loop(lower, upper, body):
    def step(i, carry):
        body(i)
        return carry

    lax.fori_loop(lower, upper, step, 0)


def kernel(
    count,
    sizes,
    g_ref,
    qr_hbm,
    ql_hbm,
    out_ref,
    gt,
    part,
    held,
    qr,
    qrt,
    ql,
    first,
    first_sum,
    share,
    second,
    leaving,
    precond,
    mine,
    all_shard,
    all_grp,
    down_send,
    up_send,
    gather_recv,
    back_send,
    back_recv,
    swap_send,
    swap_recv,
    factor_send,
    factor_recv,
    final_send,
    final_recv,
    load_sem,
    ar_send,
    ar_recv,
):
    planes, chunks = PLANES, part.shape[0]
    nb, half = g_ref.shape[0], g_ref.shape[1] // 2
    z, y = lax.axis_index("shard_0"), lax.axis_index("shard_1")
    g0, g1, g2 = lax.axis_index("grp_0"), lax.axis_index("grp_1"), lax.axis_index("grp_2")
    n1, n2 = sizes[1], sizes[2]
    n_shard, n_grp = planes * 2, sizes[0] * n1 * n2
    shard_me = z * 2 + y
    grp_me = (g0 * n1 + g1) * n2 + g2
    up_z, down_z = lax.rem(z + 1, planes), lax.rem(z + planes - 1, planes)
    own = pl.ds(pl.multiple_of(y * nb, 16), nb)
    other = pl.ds(pl.multiple_of((1 - y) * nb, 16), nb)

    def lanes(c, base=0):
        return pl.ds(pl.multiple_of(base + c * LANES, LANES), LANES)

    def shard_id(p):
        return {"shard_0": p // 2, "shard_1": lax.rem(p, 2)}

    def grp_id(p):
        return {"grp_0": p // (n1 * n2), "grp_1": lax.rem(p // n2, n1), "grp_2": lax.rem(p, n2)}

    def bottom(s, c):
        return low(s, c, chunks)

    def at_hop(h, body):
        s = z + h
        pl.when((s < planes) & (z >= bottom(s, 0)))(lambda: body(s, 0))

        @pl.when(h > 0)
        def _():
            t = lax.rem(z - h + planes, planes)
            pl.when((t > z) & (z < bottom(t, 0)))(lambda: body(t, 1))

    def load(s):
        columns = pl.ds(pl.multiple_of(s * 2 * nb, 128), 2 * nb)
        return pltpu.make_async_copy(qr_hbm.at[:, columns], qr.at[s, own], load_sem.at[s])

    load_ql = pltpu.make_async_copy(ql_hbm, ql, load_sem.at[planes])
    loop(0, HOPS + 1, lambda h: at_hop(h, lambda s, k: load(s).start()))
    load_ql.start()

    barrier = pltpu.get_barrier_semaphore()

    def greet_shard(k):
        peer = lax.rem(shard_me + k, n_shard)
        pl.semaphore_signal(barrier, inc=1, device_id=shard_id(peer), device_id_type=MESH)

    def greet_grp(k):
        peer = lax.rem(grp_me + k, n_grp)
        pl.semaphore_signal(barrier, inc=1, device_id=grp_id(peer), device_id_type=MESH)

    loop(1, n_shard, greet_shard)
    loop(1, n_grp, greet_grp)
    gt[z, own, :] = g_ref[:, pl.ds(pl.multiple_of(y * half, LANES), half)]
    pl.semaphore_wait(barrier, n_shard + n_grp - 2)

    def remote(src, dst, send, recv, to_z, to_y):
        return pltpu.make_async_remote_copy(
            src_ref=src,
            dst_ref=dst,
            send_sem=send,
            recv_sem=recv,
            device_id={"shard_0": to_z, "shard_1": to_y},
            device_id_type=MESH,
        )

    def swap(c):
        src = g_ref.at[:, lanes(c, (1 - y) * half)]
        return remote(src, gt.at[z, own, lanes(c)], swap_send.at[c], swap_recv.at[c], z, 1 - y)

    def factor(s):
        ref = qr.at[s, own]
        return remote(ref, ref, factor_send.at[s], factor_recv.at[s], z, 1 - y)

    def down(c, s):
        ref = gt.at[s, :, lanes(c)]
        return remote(ref, ref, down_send.at[c, s], gather_recv.at[c, s], down_z, y)

    def up(c, s):
        ref = gt.at[s, :, lanes(c)]
        return remote(ref, ref, up_send.at[c, s], gather_recv.at[c, s], up_z, y)

    def back(c, s, src):
        rising = (z < s) & (z >= bottom(s, c))
        parent = jnp.where(rising, up_z, down_z)
        slot = jnp.where((parent == s) & jnp.logical_not(rising), planes, s)
        return remote(src, held.at[c, slot], back_send.at[c, s], back_recv.at[c, slot], parent, y)

    def final(c):
        return remote(
            leaving.at[c], second.at[y * chunks + c], final_send.at[c], final_recv.at[c], z, 1 - y
        )

    def goes_down(c, s):
        return (z <= s) & (z - 1 >= bottom(s, c))

    def goes_up(c, s):
        return ((z >= s) & (bottom(s, c) > 0)) | ((z < s) & (z + 1 < bottom(s, c)))

    def got_back(c, slot):
        remote(held.at[c, slot], held.at[c, slot], back_send.at[0, 0], back_recv.at[c, slot], up_z, y).wait_recv()

    loop(0, chunks, lambda c: swap(c).start())

    def send_factor(s, k):
        load(s).wait()
        factor(s).start()

    loop(0, HOPS + 1, lambda h: at_hop(h, send_factor))

    def inject(c):
        @pl.when(c < chunks)
        def _():
            swap(c).wait_recv()
            pl.when(goes_down(c, z))(lambda: down(c, z).start())
            pl.when(goes_up(c, z))(lambda: up(c, z).start())

    def gather_hop(c, h):
        s = z + h

        @pl.when((c >= 0) & (c < chunks) & (s < planes) & (z >= bottom(s, c)))
        def _():
            down(c, s).wait_recv()
            pl.when(goes_down(c, s))(lambda: down(c, s).start())

        t = lax.rem(z - h + planes, planes)

        @pl.when((c >= 0) & (c < chunks) & (((z > t) & (bottom(t, c) > 0)) | ((z < t) & (z < bottom(t, c)))))
        def _():
            up(c, t).wait_recv()
            pl.when(goes_up(c, t))(lambda: up(c, t).start())

    def multiply(s, k):
        factor(s).wait_recv()
        qrt[s] = qr[s].T
        first_sum[...] += jnp.dot(qr[s], gt[s], preferred_element_type=F32)

    first_sum[...] = jnp.zeros_like(first_sum)

    def step(i):
        inject(i)
        loop(1, HOPS + 1, lambda h: gather_hop(i - h, h))
        pl.when(i >= chunks - 1)(lambda: at_hop(i - chunks + 1, multiply))

    loop(0, chunks + HOPS, step)
    first[...] = first_sum[...].astype(BF16)

    def product(s, k):
        share[k] = jnp.dot(qrt[s], first[...], preferred_element_type=F32)

    def contribute(c, s, k):
        floor = bottom(s, c)
        child = ((z >= floor) & (z - 1 >= floor)) | (z + 1 < floor)

        @pl.when(child)
        def _():
            got_back(c, s)
            part[c, s] = (share[k, :, lanes(c)] + held[c, s].astype(F32)).astype(BF16)

        @pl.when(jnp.logical_not(child))
        def _():
            part[c, s] = share[k, :, lanes(c)].astype(BF16)

        back(c, s, part.at[c, s]).start()

    def back_phase(i):
        h = HOPS - i
        at_hop(h, product)

        def send(c):
            at_hop(h, lambda s, k: contribute(c, s, k))
            t = z - h

            @pl.when((t >= 0) & (bottom(t, c) > 0))
            def _():
                got_back(c, t)
                back(c, t, held.at[c, t]).start()

        loop(0, chunks, send)

    loop(0, HOPS, back_phase)

    product(z, 0)

    def finish(c):
        @pl.when(z > 0)
        def _():
            got_back(c, z)
            share[0, :, lanes(c)] += held[c, z].astype(F32)

        @pl.when(bottom(z, c) > 0)
        def _():
            got_back(c, planes)
            share[0, :, lanes(c)] += held[c, planes].astype(F32)

        leaving[c] = share[0, other, lanes(c)].astype(BF16)
        final(c).start()
        second[y * chunks + c] = share[0, own, lanes(c)].astype(BF16)

    loop(0, chunks, finish)

    load_ql.wait()
    loop(0, chunks, lambda c: final(c).wait_recv())
    sub = jnp.concatenate([second[c] for c in range(2 * chunks)], axis=1)
    third = lax.dot_general(sub, ql[...], (((1,), (1,)), ((), ())), preferred_element_type=F32).astype(BF16)
    precond[...] = jnp.dot(third, ql[...], preferred_element_type=F32)

    value = precond[...]
    square = value * value
    tile = square[0:8]
    for r in range(8, nb, 8):
        tile = tile + square[r : r + 8]
    total = tile[:, 0:128]
    for k in range(128, value.shape[1], 128):
        total = total + tile[:, k : k + 128]
    mine[...] = total

    def exchange(phase, n, me, ident, slots):
        slots[me] = mine[...]

        def make(peer, at):
            return pltpu.make_async_remote_copy(
                src_ref=mine,
                dst_ref=slots.at[at],
                send_sem=ar_send.at[phase, peer],
                recv_sem=ar_recv.at[phase, at],
                device_id=ident(peer),
                device_id_type=MESH,
            )

        loop(1, n, lambda k: make(lax.rem(me + k, n), me).start())

        def wait(k):
            peer = lax.rem(me + k, n)
            make(peer, peer).wait_recv()

        loop(1, n, wait)
        loop(1, n, lambda k: make(lax.rem(me + k, n), me).wait_send())
        total = slots[0]
        for k in range(1, n):
            total = total + slots[k]
        mine[...] = total

    exchange(0, n_shard, shard_me, shard_id, all_shard)
    exchange(1, n_grp, grp_me, grp_id, all_grp)

    rms = jnp.sqrt(jnp.sum(mine[...], keepdims=True) / count + 1e-06)
    scale = jnp.minimum(jnp.float32(1.0), 1.1 / rms)
    out_ref[...] = (precond[...] * scale).astype(BF16)

    def drain(c):
        swap(c).wait_send()
        final(c).wait_send()

        def each(s):
            pl.when(goes_down(c, s))(lambda: down(c, s).wait_send())
            pl.when(goes_up(c, s))(lambda: up(c, s).wait_send())
            pl.when((z < s) | ((z > s) & (bottom(s, c) > 0)))(lambda: back(c, s, part.at[c, s]).wait_send())

        loop(0, planes, each)

    loop(0, chunks, drain)
    loop(z, planes, lambda s: factor(s).wait_send())


def body(sizes, gradients, left_factor, right_factor):
    rows, nb = gradients.shape[1:]
    half = rows // 2
    chunks = half // LANES
    planes = PLANES
    n_shard, n_grp = 2 * planes, sizes[0] * sizes[1] * sizes[2]
    count = gradients.shape[0] * n_grp * rows * nb * n_shard
    dma = pltpu.SemaphoreType.DMA
    turned = pl.pallas_call(
        functools.partial(kernel, count, sizes),
        out_shape=jax.ShapeDtypeStruct((nb, rows), BF16),
        in_specs=[
            pl.BlockSpec(memory_space=pltpu.VMEM),
            pl.BlockSpec(memory_space=pl.ANY),
            pl.BlockSpec(memory_space=pl.ANY),
        ],
        out_specs=pl.BlockSpec(memory_space=pltpu.VMEM),
        scratch_shapes=[
            pltpu.VMEM((planes, 2 * nb, half), BF16),
            pltpu.VMEM((chunks, planes, 2 * nb, LANES), BF16),
            pltpu.VMEM((chunks, planes + 1, 2 * nb, LANES), BF16),
            pltpu.VMEM((planes, 2 * nb, 2 * nb), BF16),
            pltpu.VMEM((planes, 2 * nb, 2 * nb), BF16),
            pltpu.VMEM((rows, rows), BF16),
            pltpu.VMEM((2 * nb, half), BF16),
            pltpu.VMEM((2 * nb, half), F32),
            pltpu.VMEM((2, 2 * nb, half), F32),
            pltpu.VMEM((2 * chunks, nb, LANES), BF16),
            pltpu.VMEM((chunks, nb, LANES), BF16),
            pltpu.VMEM((nb, rows), F32),
            pltpu.VMEM((8, 128), F32),
            pltpu.VMEM((n_shard, 8, 128), F32),
            pltpu.VMEM((n_grp, 8, 128), F32),
            dma((chunks, planes)),
            dma((chunks, planes)),
            dma((chunks, planes)),
            dma((chunks, planes)),
            dma((chunks, planes + 1)),
            dma((chunks,)),
            dma((chunks,)),
            dma((planes,)),
            dma((planes,)),
            dma((chunks,)),
            dma((chunks,)),
            dma((planes + 1,)),
            dma((2, max(n_shard, n_grp))),
            dma((2, max(n_shard, n_grp))),
        ],
        compiler_params=pltpu.CompilerParams(
            collective_id=0, has_side_effects=True, vmem_limit_bytes=67043328
        ),
        name="precondition",
    )(gradients[0].T, right_factor[0], left_factor[0])
    return turned.T[None]


def split_mesh(devices, sizes):
    return Mesh(devices.reshape(*sizes, PLANES, 2), GRP + SHARD)


def program(split, sizes):
    in_specs = (P(GRP, None, SHARD), P(GRP, None, None), P(GRP, SHARD, None))
    return jax.shard_map(
        functools.partial(body, sizes), mesh=split, in_specs=in_specs, out_specs=P(GRP, None, SHARD), check_vma=False
    )


def solution(mesh):
    sizes = (2, 4, 2)
    return program(split_mesh(mesh.devices, sizes), sizes)
```

time: 205 us -> 164 us (0.80)
  Pallas kernels: 200 us -> 162 us
  local copies, waits for them, and re-layouts: 4.2 us -> 1.97 us
    pallas_call x1, Pallas kernels: 200 us -> 162 us  [body(): pl.pallas_call(functools.partial(kernel, count, sizes), out_shape=jax.Sha...]
    unnamed x2 -> x1, local copies, waits for them, and re-layouts: 4.2 us -> 1.97 us
where the time goes in v2:
time: 164 us
  Pallas kernels  162 us (99%)
  local copies, waits for them, and re-layouts  1.97 us (1%)
    pallas_call x1, Pallas kernels, body(): pl.pallas_call(functools.partial(kernel, count, sizes), out_shape=jax.Sha...  162 us

profile of v2, /device:TPU:1, one launch (start us, length us, event | category | flops | bytes accessed | tf_op | source)
XLA Modules:
  0.0 163.7 jit_solution(10086007510941993240)
XLA Ops:
  0.0 161.7 %precondition.1 = bf16[320,1024]{1,0:T(8,128)(2,1)} custom-call(bf16[320,1024]{1,0:T(8,128)(2,1)} %bitcast.11, bf16[320,5120]{1,0:T(8,128)(2,1)} %bitcast.8, bf16[1024,1024]{1,0:T(8,128)(2,1)} %bitcast.10), custom_call_target="tpu_custom_call" | custom-call | tf_op jit(solution)/shard_map/precondition/pallas_call | solution.py:344
  161.7 2.0 %copy.5 = bf16[1,1024,320]{1,2,0:T(8,128)(2,1)} copy(bf16[1,1024,320]{1,2,0:T(8,128)(2,1)} %bitcast.9) | data formatting | bytes 1310720

commit v3 on v2

--- a/solution.py
+++ b/solution.py
@@ -49,6 +49,8 @@
     share,
     second,
     leaving,
+    relay_in,
+    relay_out,
     precond,
     mine,
     all_shard,
@@ -56,12 +58,16 @@
     down_send,
     up_send,
     gather_recv,
+    piece_send,
+    piece_recv,
     back_send,
     back_recv,
     swap_send,
     swap_recv,
     factor_send,
     factor_recv,
+    relay_send,
+    relay_recv,
     final_send,
     final_recv,
     load_sem,
@@ -161,61 +167,125 @@
             leaving.at[c], second.at[y * chunks + c], final_send.at[c], final_recv.at[c], z, 1 - y
         )
 
-    def goes_down(c, s):
-        return (z <= s) & (z - 1 >= bottom(s, c))
-
-    def goes_up(c, s):
-        return ((z >= s) & (bottom(s, c) > 0)) | ((z < s) & (z + 1 < bottom(s, c)))
+    def goes_down(s):
+        return (z <= s) & (z - 1 >= bottom(s, 0))
+
+    def goes_up(s):
+        return ((z >= s) & (bottom(s, 0) > 0)) | ((z < s) & (z + 1 < bottom(s, 0)))
 
     def got_back(c, slot):
         remote(held.at[c, slot], held.at[c, slot], back_send.at[0, 0], back_recv.at[c, slot], up_z, y).wait_recv()
 
-    loop(0, chunks, lambda c: swap(c).start())
+    def relayed(s):
+        return ((z <= 2) & (s == z + 4)) | ((z == 0) & (s == 5))
+
+    def relays(k):
+        return (z == 7) | ((k == 0) & ((z == 2) | (z == 3)))
+
+    def relay_slot(s):
+        return jnp.where((z == 0) & (s == 4), 1, 0)
+
+    def relay_first(s, k):
+        via = jnp.where(z == 0, down_z, up_z)
+        return remote(qr.at[s, own], relay_in.at[k], relay_send.at[0, k], relay_recv.at[0, k], via, y)
+
+    def relay_second(k):
+        return remote(relay_in.at[k], relay_out.at[k], relay_send.at[1, k], relay_recv.at[1, k], z, 1 - y)
+
+    def relay_third(k):
+        s = jnp.where(z == 7, 5 - k, z + 3)
+        to = jnp.where(z == 7, up_z, down_z)
+        return remote(relay_out.at[k], qr.at[s, other], relay_send.at[2, k], factor_recv.at[s], to, y)
+
+    def start_relay(s, k):
+        @pl.when(relayed(s))
+        def _():
+            load(s).wait()
+            relay_first(s, relay_slot(s)).start()
 
     def send_factor(s, k):
-        load(s).wait()
-        factor(s).start()
-
-    loop(0, HOPS + 1, lambda h: at_hop(h, send_factor))
+        @pl.when(jnp.logical_not(relayed(s)))
+        def _():
+            load(s).wait()
+            factor(s).start()
+
+    def relay_on(k):
+        @pl.when(relays(k))
+        def _():
+            relay_first(z, k).wait_recv()
+            relay_second(k).start()
+
+    def relay_home(k):
+        @pl.when(relays(k))
+        def _():
+            relay_second(k).wait_recv()
+            relay_third(k).start()
+
+    def piece(c, way, k, s):
+        ref = gt.at[s, own if k == 0 else other, lanes(c)]
+        return remote(ref, ref, piece_send.at[way, k, c], piece_recv.at[way, k, c], (down_z, up_z)[way], y)
+
+    def start_pieces(c, k):
+        pl.when(goes_down(z))(lambda: piece(c, 0, k, z).start())
+        pl.when(goes_up(z))(lambda: piece(c, 1, k, z).start())
 
     def inject(c):
-        @pl.when(c < chunks)
-        def _():
-            swap(c).wait_recv()
-            pl.when(goes_down(c, z))(lambda: down(c, z).start())
-            pl.when(goes_up(c, z))(lambda: up(c, z).start())
-
-    def gather_hop(c, h):
-        s = z + h
-
-        @pl.when((c >= 0) & (c < chunks) & (s < planes) & (z >= bottom(s, c)))
-        def _():
-            down(c, s).wait_recv()
-            pl.when(goes_down(c, s))(lambda: down(c, s).start())
-
-        t = lax.rem(z - h + planes, planes)
-
-        @pl.when((c >= 0) & (c < chunks) & (((z > t) & (bottom(t, c) > 0)) | ((z < t) & (z < bottom(t, c)))))
-        def _():
-            up(c, t).wait_recv()
-            pl.when(goes_up(c, t))(lambda: up(c, t).start())
+        swap(c).wait_recv()
+        start_pieces(c, 1)
+
+    def gather_hop(h, arrive):
+        def chunk(c):
+            s = z + h
+
+            @pl.when((s < planes) & (z >= bottom(s, 0)))
+            def _():
+                arrive(c, 0, s)
+                pl.when(goes_down(s))(lambda: down(c, s).start())
+
+            t = lax.rem(z - h + planes, planes)
+
+            @pl.when(((z > t) & (bottom(t, 0) > 0)) | ((z < t) & (z < bottom(t, 0))))
+            def _():
+                arrive(c, 1, t)
+                pl.when(goes_up(t))(lambda: up(c, t).start())
+
+        loop(0, chunks, chunk)
+
+    def arrive_pieces(c, way, s):
+        piece(c, way, 0, s).wait_recv()
+        piece(c, way, 1, s).wait_recv()
+
+    def arrive_whole(c, way, s):
+        down(c, s).wait_recv()
 
     def multiply(s, k):
         factor(s).wait_recv()
+        first_sum[...] += jnp.dot(qr[s], gt[s], preferred_element_type=F32)
+
+    loop(0, chunks, lambda c: swap(c).start())
+    at_hop(0, send_factor)
+    loop(HOPS - 1, HOPS + 1, lambda h: at_hop(h, start_relay))
+    loop(0, chunks, lambda c: start_pieces(c, 0))
+    loop(0, chunks, inject)
+    relay_on(0)
+    loop(1, HOPS + 1, lambda h: at_hop(h, send_factor))
+    first_sum[...] = jnp.zeros_like(first_sum)
+    gather_hop(1, arrive_pieces)
+    relay_on(1)
+    relay_home(0)
+    at_hop(0, multiply)
+
+    def hop(h):
+        gather_hop(h, arrive_whole)
+        pl.when(h == 2)(lambda: relay_home(1))
+        at_hop(h - 1, multiply)
+
+    loop(2, HOPS + 1, hop)
+    at_hop(HOPS, multiply)
+    first[...] = first_sum[...].astype(BF16)
+
+    def product(s, k):
         qrt[s] = qr[s].T
-        first_sum[...] += jnp.dot(qr[s], gt[s], preferred_element_type=F32)
-
-    first_sum[...] = jnp.zeros_like(first_sum)
-
-    def step(i):
-        inject(i)
-        loop(1, HOPS + 1, lambda h: gather_hop(i - h, h))
-        pl.when(i >= chunks - 1)(lambda: at_hop(i - chunks + 1, multiply))
-
-    loop(0, chunks + HOPS, step)
-    first[...] = first_sum[...].astype(BF16)
-
-    def product(s, k):
         share[k] = jnp.dot(qrt[s], first[...], preferred_element_type=F32)
 
     def contribute(c, s, k):
@@ -321,16 +391,31 @@
     def drain(c):
         swap(c).wait_send()
         final(c).wait_send()
+        for k in range(2):
+            pl.when(goes_down(z))(lambda: piece(c, 0, k, z).wait_send())
+            pl.when(goes_up(z))(lambda: piece(c, 1, k, z).wait_send())
 
         def each(s):
-            pl.when(goes_down(c, s))(lambda: down(c, s).wait_send())
-            pl.when(goes_up(c, s))(lambda: up(c, s).wait_send())
+            pl.when(goes_down(s) & (s != z))(lambda: down(c, s).wait_send())
+            pl.when(goes_up(s) & (s != z))(lambda: up(c, s).wait_send())
             pl.when((z < s) | ((z > s) & (bottom(s, c) > 0)))(lambda: back(c, s, part.at[c, s]).wait_send())
 
         loop(0, planes, each)
 
     loop(0, chunks, drain)
-    loop(z, planes, lambda s: factor(s).wait_send())
+
+    def drain_factor(s):
+        pl.when(relayed(s))(lambda: relay_first(s, relay_slot(s)).wait_send())
+        pl.when(jnp.logical_not(relayed(s)))(lambda: factor(s).wait_send())
+
+    def drain_relay(k):
+        @pl.when(relays(k))
+        def _():
+            relay_second(k).wait_send()
+            relay_third(k).wait_send()
+
+    loop(z, planes, drain_factor)
+    loop(0, 2, drain_relay)
 
 
 def body(sizes, gradients, left_factor, right_factor):
@@ -362,6 +447,8 @@
             pltpu.VMEM((2, 2 * nb, half), F32),
             pltpu.VMEM((2 * chunks, nb, LANES), BF16),
             pltpu.VMEM((chunks, nb, LANES), BF16),
+            pltpu.VMEM((2, nb, 2 * nb), BF16),
+            pltpu.VMEM((2, nb, 2 * nb), BF16),
             pltpu.VMEM((nb, rows), F32),
             pltpu.VMEM((8, 128), F32),
             pltpu.VMEM((n_shard, 8, 128), F32),
@@ -369,12 +456,16 @@
             dma((chunks, planes)),
             dma((chunks, planes)),
             dma((chunks, planes)),
+            dma((2, 2, chunks)),
+            dma((2, 2, chunks)),
             dma((chunks, planes)),
             dma((chunks, planes + 1)),
             dma((chunks,)),
             dma((chunks,)),
             dma((planes,)),
             dma((planes,)),
+            dma((3, 2)),
+            dma((2, 2)),
             dma((chunks,)),
             dma((chunks,)),
             dma((planes + 1,)),

time: 164 us -> 148 us (0.902)
  Pallas kernels: 162 us -> 146 us
    pallas_call x1, Pallas kernels: 162 us -> 146 us  [body(): pl.pallas_call(functools.partial(kernel, count, sizes), out_shape=jax.Sha...]
where the time goes in v3:
time: 148 us
  Pallas kernels  146 us (99%)
  local copies, waits for them, and re-layouts  1.97 us (1%)
    pallas_call x1, Pallas kernels, body(): pl.pallas_call(functools.partial(kernel, count, sizes), out_shape=jax.Sha...  146 us

profile of v3, /device:TPU:1, one launch (start us, length us, event | category | flops | bytes accessed | tf_op | source)
XLA Modules:
  0.0 147.9 jit_solution(16084287496769972026)
XLA Ops:
  0.0 145.9 %precondition.1 = bf16[320,1024]{1,0:T(8,128)(2,1)} custom-call(bf16[320,1024]{1,0:T(8,128)(2,1)} %bitcast.11, bf16[320,5120]{1,0:T(8,128)(2,1)} %bitcast.8, bf16[1024,1024]{1,0:T(8,128)(2,1)} %bitcast.10), custom_call_target="tpu_custom_call" | custom-call | tf_op jit(solution)/shard_map/precondition/pallas_call | solution.py:429
  145.9 2.0 %copy.5 = bf16[1,1024,320]{1,2,0:T(8,128)(2,1)} copy(bf16[1,1024,320]{1,2,0:T(8,128)(2,1)} %bitcast.9) | data formatting | bytes 1310720

commit v4 on v3

--- a/solution.py
+++ b/solution.py
@@ -49,6 +49,10 @@
     share,
     second,
     leaving,
+    coming,
+    kept,
+    landed,
+    swapped,
     relay_in,
     relay_out,
     precond,
@@ -62,6 +66,8 @@
     piece_recv,
     back_send,
     back_recv,
+    last_send,
+    landed_recv,
     swap_send,
     swap_recv,
     factor_send,
@@ -75,7 +81,7 @@
     ar_recv,
 ):
     planes, chunks = PLANES, part.shape[0]
-    nb, half = g_ref.shape[0], g_ref.shape[1] // 2
+    nb, half = leaving.shape[1], first.shape[1]
     z, y = lax.axis_index("shard_0"), lax.axis_index("shard_1")
     g0, g1, g2 = lax.axis_index("grp_0"), lax.axis_index("grp_1"), lax.axis_index("grp_2")
     n1, n2 = sizes[1], sizes[2]
@@ -112,6 +118,12 @@
         return pltpu.make_async_copy(qr_hbm.at[:, columns], qr.at[s, own], load_sem.at[s])
 
     load_ql = pltpu.make_async_copy(ql_hbm, ql, load_sem.at[planes])
+    mine_half = pl.ds(pl.multiple_of(y * half, LANES), half)
+    swap_half = pl.ds(pl.multiple_of((1 - y) * half, LANES), half)
+    load_mine = pltpu.make_async_copy(g_ref.at[:, mine_half], gt.at[z, own], load_sem.at[planes + 1])
+    load_swap = pltpu.make_async_copy(g_ref.at[:, swap_half], swapped, load_sem.at[planes + 2])
+    load_swap.start()
+    load_mine.start()
     loop(0, HOPS + 1, lambda h: at_hop(h, lambda s, k: load(s).start()))
     load_ql.start()
 
@@ -127,7 +139,8 @@
 
     loop(1, n_shard, greet_shard)
     loop(1, n_grp, greet_grp)
-    gt[z, own, :] = g_ref[:, pl.ds(pl.multiple_of(y * half, LANES), half)]
+    load_swap.wait()
+    load_mine.wait()
     pl.semaphore_wait(barrier, n_shard + n_grp - 2)
 
     def remote(src, dst, send, recv, to_z, to_y):
@@ -141,8 +154,7 @@
         )
 
     def swap(c):
-        src = g_ref.at[:, lanes(c, (1 - y) * half)]
-        return remote(src, gt.at[z, own, lanes(c)], swap_send.at[c], swap_recv.at[c], z, 1 - y)
+        return remote(swapped.at[:, lanes(c)], gt.at[z, own, lanes(c)], swap_send.at[c], swap_recv.at[c], z, 1 - y)
 
     def factor(s):
         ref = qr.at[s, own]
@@ -159,13 +171,19 @@
     def back(c, s, src):
         rising = (z < s) & (z >= bottom(s, c))
         parent = jnp.where(rising, up_z, down_z)
-        slot = jnp.where((parent == s) & jnp.logical_not(rising), planes, s)
-        return remote(src, held.at[c, slot], back_send.at[c, s], back_recv.at[c, slot], parent, y)
+        return remote(src, held.at[c, s], back_send.at[c, s], back_recv.at[c, s], parent, y)
+
+    def last(c, way, k, src):
+        to_z = (up_z, down_z)[way]
+        send, recv = last_send.at[way, k, c], landed_recv.at[way, y, c]
+        return remote(src, landed.at[way, y, c], send, recv, to_z, y if k == 0 else 1 - y)
+
+    def start_last(c, way, ref):
+        last(c, way, 0, ref.at[own]).start()
+        last(c, way, 1, ref.at[other]).start()
 
     def final(c):
-        return remote(
-            leaving.at[c], second.at[y * chunks + c], final_send.at[c], final_recv.at[c], z, 1 - y
-        )
+        return remote(leaving.at[c], coming.at[c], final_send.at[c], final_recv.at[c], z, 1 - y)
 
     def goes_down(s):
         return (z <= s) & (z - 1 >= bottom(s, 0))
@@ -173,8 +191,8 @@
     def goes_up(s):
         return ((z >= s) & (bottom(s, 0) > 0)) | ((z < s) & (z + 1 < bottom(s, 0)))
 
-    def got_back(c, slot):
-        remote(held.at[c, slot], held.at[c, slot], back_send.at[0, 0], back_recv.at[c, slot], up_z, y).wait_recv()
+    def got_back(c, s):
+        remote(held.at[c, s], held.at[c, s], back_send.at[0, 0], back_recv.at[c, s], up_z, y).wait_recv()
 
     def relayed(s):
         return ((z <= 2) & (s == z + 4)) | ((z == 0) & (s == 5))
@@ -258,9 +276,12 @@
     def arrive_whole(c, way, s):
         down(c, s).wait_recv()
 
-    def multiply(s, k):
+    def multiply_own(s, k):
+        first_sum[own, :] += jnp.dot(qr[s, own, :], gt[s], preferred_element_type=F32)
+
+    def multiply_other(s, k):
         factor(s).wait_recv()
-        first_sum[...] += jnp.dot(qr[s], gt[s], preferred_element_type=F32)
+        first_sum[other, :] += jnp.dot(qr[s, other, :], gt[s], preferred_element_type=F32)
 
     loop(0, chunks, lambda c: swap(c).start())
     at_hop(0, send_factor)
@@ -273,22 +294,25 @@
     gather_hop(1, arrive_pieces)
     relay_on(1)
     relay_home(0)
-    at_hop(0, multiply)
+    at_hop(0, multiply_own)
+    at_hop(1, multiply_own)
+    at_hop(0, multiply_other)
 
     def hop(h):
         gather_hop(h, arrive_whole)
         pl.when(h == 2)(lambda: relay_home(1))
-        at_hop(h - 1, multiply)
+        at_hop(h, multiply_own)
+        at_hop(h - 1, multiply_other)
 
     loop(2, HOPS + 1, hop)
-    at_hop(HOPS, multiply)
+    at_hop(HOPS, multiply_other)
     first[...] = first_sum[...].astype(BF16)
 
     def product(s, k):
         qrt[s] = qr[s].T
         share[k] = jnp.dot(qrt[s], first[...], preferred_element_type=F32)
 
-    def contribute(c, s, k):
+    def contribute(c, s, k, send):
         floor = bottom(s, c)
         child = ((z >= floor) & (z - 1 >= floor)) | (z + 1 < floor)
 
@@ -301,46 +325,74 @@
         def _():
             part[c, s] = share[k, :, lanes(c)].astype(BF16)
 
-        back(c, s, part.at[c, s]).start()
-
-    def back_phase(i):
-        h = HOPS - i
+        send(c, s, k, part.at[c, s])
+
+    def back_phase(h, send):
         at_hop(h, product)
 
-        def send(c):
-            at_hop(h, lambda s, k: contribute(c, s, k))
+        def chunk(c):
+            at_hop(h, lambda s, k: contribute(c, s, k, send))
             t = z - h
 
             @pl.when((t >= 0) & (bottom(t, c) > 0))
             def _():
                 got_back(c, t)
-                back(c, t, held.at[c, t]).start()
-
-        loop(0, chunks, send)
-
-    loop(0, HOPS, back_phase)
+                send(c, t, 1, held.at[c, t])
+
+        loop(0, chunks, chunk)
+
+    def send_back(c, s, k, ref):
+        back(c, s, ref).start()
+
+    def send_last(c, s, k, ref):
+        start_last(c, k, ref)
+
+    loop(0, HOPS - 2, lambda i: back_phase(HOPS - i, send_back))
 
     product(z, 0)
+    kept[...] = share[0, own, :]
+
+    def leave(c):
+        leaving[c] = share[0, other, lanes(c)]
+        final(c).start()
+
+    loop(0, chunks, leave)
+    back_phase(2, send_back)
+    back_phase(1, send_last)
+
+    def arrived(way, line, c):
+        return remote(
+            landed.at[way, line, c],
+            landed.at[way, line, c],
+            last_send.at[0, 0, 0],
+            landed_recv.at[way, line, c],
+            up_z,
+            y,
+        )
 
     def finish(c):
+        final(c).wait_recv()
+
         @pl.when(z > 0)
         def _():
-            got_back(c, z)
-            share[0, :, lanes(c)] += held[c, z].astype(F32)
+            arrived(0, y, c).wait_recv()
+            arrived(0, 1 - y, c).wait_recv()
+            kept[:, lanes(c)] += landed[0, y, c].astype(F32)
+            coming[c] += landed[0, 1 - y, c].astype(F32)
 
         @pl.when(bottom(z, c) > 0)
         def _():
-            got_back(c, planes)
-            share[0, :, lanes(c)] += held[c, planes].astype(F32)
-
-        leaving[c] = share[0, other, lanes(c)].astype(BF16)
-        final(c).start()
-        second[y * chunks + c] = share[0, own, lanes(c)].astype(BF16)
+            arrived(1, y, c).wait_recv()
+            arrived(1, 1 - y, c).wait_recv()
+            kept[:, lanes(c)] += landed[1, y, c].astype(F32)
+            coming[c] += landed[1, 1 - y, c].astype(F32)
+
+        second[y * chunks + c] = kept[:, lanes(c)].astype(BF16)
+        second[(1 - y) * chunks + c] = coming[c].astype(BF16)
 
     loop(0, chunks, finish)
 
     load_ql.wait()
-    loop(0, chunks, lambda c: final(c).wait_recv())
     sub = jnp.concatenate([second[c] for c in range(2 * chunks)], axis=1)
     third = lax.dot_general(sub, ql[...], (((1,), (1,)), ((), ())), preferred_element_type=F32).astype(BF16)
     precond[...] = jnp.dot(third, ql[...], preferred_element_type=F32)
@@ -394,11 +446,16 @@
         for k in range(2):
             pl.when(goes_down(z))(lambda: piece(c, 0, k, z).wait_send())
             pl.when(goes_up(z))(lambda: piece(c, 1, k, z).wait_send())
+            pl.when(z < planes - 1)(lambda: last(c, 0, k, part.at[c, 0, own]).wait_send())
+            falls = (z == 0) | (bottom(z - 1, c) > 0)
+            pl.when(falls)(lambda: last(c, 1, k, part.at[c, 0, own]).wait_send())
 
         def each(s):
             pl.when(goes_down(s) & (s != z))(lambda: down(c, s).wait_send())
             pl.when(goes_up(s) & (s != z))(lambda: up(c, s).wait_send())
-            pl.when((z < s) | ((z > s) & (bottom(s, c) > 0)))(lambda: back(c, s, part.at[c, s]).wait_send())
+            comes = (z < s) | ((z > s) & (bottom(s, c) > 0))
+            near = (s == z + 1) | (s == down_z)
+            pl.when(comes & jnp.logical_not(near))(lambda: back(c, s, part.at[c, s]).wait_send())
 
         loop(0, planes, each)
 
@@ -430,7 +487,7 @@
         functools.partial(kernel, count, sizes),
         out_shape=jax.ShapeDtypeStruct((nb, rows), BF16),
         in_specs=[
-            pl.BlockSpec(memory_space=pltpu.VMEM),
+            pl.BlockSpec(memory_space=pl.ANY),
             pl.BlockSpec(memory_space=pl.ANY),
             pl.BlockSpec(memory_space=pl.ANY),
         ],
@@ -438,7 +495,7 @@
         scratch_shapes=[
             pltpu.VMEM((planes, 2 * nb, half), BF16),
             pltpu.VMEM((chunks, planes, 2 * nb, LANES), BF16),
-            pltpu.VMEM((chunks, planes + 1, 2 * nb, LANES), BF16),
+            pltpu.VMEM((chunks, planes, 2 * nb, LANES), BF16),
             pltpu.VMEM((planes, 2 * nb, 2 * nb), BF16),
             pltpu.VMEM((planes, 2 * nb, 2 * nb), BF16),
             pltpu.VMEM((rows, rows), BF16),
@@ -446,7 +503,11 @@
             pltpu.VMEM((2 * nb, half), F32),
             pltpu.VMEM((2, 2 * nb, half), F32),
             pltpu.VMEM((2 * chunks, nb, LANES), BF16),
-            pltpu.VMEM((chunks, nb, LANES), BF16),
+            pltpu.VMEM((chunks, nb, LANES), F32),
+            pltpu.VMEM((chunks, nb, LANES), F32),
+            pltpu.VMEM((nb, half), F32),
+            pltpu.VMEM((2, 2, chunks, nb, LANES), BF16),
+            pltpu.VMEM((nb, half), BF16),
             pltpu.VMEM((2, nb, 2 * nb), BF16),
             pltpu.VMEM((2, nb, 2 * nb), BF16),
             pltpu.VMEM((nb, rows), F32),
@@ -459,7 +520,9 @@
             dma((2, 2, chunks)),
             dma((2, 2, chunks)),
             dma((chunks, planes)),
-            dma((chunks, planes + 1)),
+            dma((chunks, planes)),
+            dma((2, 2, chunks)),
+            dma((2, 2, chunks)),
             dma((chunks,)),
             dma((chunks,)),
             dma((planes,)),
@@ -468,7 +531,7 @@
             dma((2, 2)),
             dma((chunks,)),
             dma((chunks,)),
-            dma((planes + 1,)),
+            dma((planes + 3,)),
             dma((2, max(n_shard, n_grp))),
             dma((2, max(n_shard, n_grp))),
         ],

time: 148 us -> 144 us (0.973)
  Pallas kernels: 146 us -> 142 us
    pallas_call x1, Pallas kernels: 146 us -> 142 us  [body(): pl.pallas_call(functools.partial(kernel, count, sizes), out_shape=jax.Sha...]
where the time goes in v4:
time: 144 us
  Pallas kernels  142 us (99%)
  local copies, waits for them, and re-layouts  1.97 us (1%)
    pallas_call x1, Pallas kernels, body(): pl.pallas_call(functools.partial(kernel, count, sizes), out_shape=jax.Sha...  142 us

profile of v4, /device:TPU:1, one launch (start us, length us, event | category | flops | bytes accessed | tf_op | source)
XLA Modules:
  0.0 143.8 jit_solution(6914346174622453577)
XLA Ops:
  0.0 141.8 %precondition.1 = bf16[320,1024]{1,0:T(8,128)(2,1)} custom-call(bf16[320,1024]{1,0:T(8,128)(2,1)} %bitcast.11, bf16[320,5120]{1,0:T(8,128)(2,1)} %bitcast.8, bf16[1024,1024]{1,0:T(8,128)(2,1)} %bitcast.10), custom_call_target="tpu_custom_call" | custom-call | tf_op jit(solution)/shard_map/precondition/pallas_call | solution.py:486
  141.8 2.0 %copy.5 = bf16[1,1024,320]{1,2,0:T(8,128)(2,1)} copy(bf16[1,1024,320]{1,2,0:T(8,128)(2,1)} %bitcast.9) | data formatting | bytes 1310720

commit v5 on v4

--- a/solution.py
+++ b/solution.py
@@ -77,6 +77,7 @@
     final_send,
     final_recv,
     load_sem,
+    chain_sem,
     ar_send,
     ar_recv,
 ):
@@ -129,19 +130,28 @@
 
     barrier = pltpu.get_barrier_semaphore()
 
-    def greet_shard(k):
-        peer = lax.rem(shard_me + k, n_shard)
-        pl.semaphore_signal(barrier, inc=1, device_id=shard_id(peer), device_id_type=MESH)
-
-    def greet_grp(k):
-        peer = lax.rem(grp_me + k, n_grp)
-        pl.semaphore_signal(barrier, inc=1, device_id=grp_id(peer), device_id_type=MESH)
-
-    loop(1, n_shard, greet_shard)
-    loop(1, n_grp, greet_grp)
+    def greet(semaphore, ids):
+        for peer in ids:
+            pl.semaphore_signal(semaphore, inc=1, device_id=peer, device_id_type=MESH)
+
+    x_ids = [{"grp_1": lax.rem(g1 + k, n1)} for k in (1, n1 - 1)] if n1 > 1 else []
+    y_ids = [{"shard_1": 1 - y}] + ([{"grp_0": 1 - g0, "shard_1": 1 - y}] if sizes[0] > 1 else [])
+    core_ids = [{"grp_2": 1 - g2}] if n2 > 1 else []
+    z_ids = [{"shard_0": to, "shard_1": line} for to in (up_z, down_z) for line in (y, 1 - y)]
+    greet(barrier, y_ids + z_ids + x_ids + core_ids)
     load_swap.wait()
     load_mine.wait()
-    pl.semaphore_wait(barrier, n_shard + n_grp - 2)
+    pl.semaphore_wait(barrier, len(y_ids) + len(z_ids) + len(x_ids) + len(core_ids))
+
+    chain = [y_ids, x_ids, x_ids, core_ids]
+
+    def pass_on(k):
+        if k > 0:
+            pl.semaphore_wait(chain_sem.at[k - 1], len(chain[k - 1])) if chain[k - 1] else None
+        if k < len(chain):
+            greet(chain_sem.at[k], chain[k])
+
+    pass_on(0)
 
     def remote(src, dst, send, recv, to_z, to_y):
         return pltpu.make_async_remote_copy(
@@ -290,10 +300,12 @@
     loop(0, chunks, inject)
     relay_on(0)
     loop(1, HOPS + 1, lambda h: at_hop(h, send_factor))
+    pass_on(1)
     first_sum[...] = jnp.zeros_like(first_sum)
     gather_hop(1, arrive_pieces)
     relay_on(1)
     relay_home(0)
+    pass_on(2)
     at_hop(0, multiply_own)
     at_hop(1, multiply_own)
     at_hop(0, multiply_other)
@@ -308,6 +320,8 @@
     at_hop(HOPS, multiply_other)
     first[...] = first_sum[...].astype(BF16)
 
+    pass_on(3)
+
     def product(s, k):
         qrt[s] = qr[s].T
         share[k] = jnp.dot(qrt[s], first[...], preferred_element_type=F32)
@@ -348,6 +362,8 @@
         start_last(c, k, ref)
 
     loop(0, HOPS - 2, lambda i: back_phase(HOPS - i, send_back))
+
+    pass_on(4)
 
     product(z, 0)
     kept[...] = share[0, own, :]
@@ -532,6 +548,7 @@
             dma((chunks,)),
             dma((chunks,)),
             dma((planes + 3,)),
+            pltpu.SemaphoreType.REGULAR((4,)),
             dma((2, max(n_shard, n_grp))),
             dma((2, max(n_shard, n_grp))),
         ],

time: 144 us -> 143 us (level)
  Pallas kernels: 142 us -> 140 us
where the time goes in v5:
time: 143 us; the launch traced here: 142 us
  Pallas kernels  140 us (98%)
  local copies, waits for them, and re-layouts  1.97 us (1%)
    pallas_call x1, Pallas kernels, body(): pl.pallas_call(functools.partial(kernel, count, sizes), out_shape=jax.Sha...  140 us

profile of v5, /device:TPU:1, one launch (start us, length us, event | category | flops | bytes accessed | tf_op | source)
XLA Modules:
  0.0 142.5 jit_solution(17160368195165244964)
XLA Ops:
  0.0 140.5 %precondition.1 = bf16[320,1024]{1,0:T(8,128)(2,1)} custom-call(bf16[320,1024]{1,0:T(8,128)(2,1)} %bitcast.11, bf16[320,5120]{1,0:T(8,128)(2,1)} %bitcast.8, bf16[1024,1024]{1,0:T(8,128)(2,1)} %bitcast.10), custom_call_target="tpu_custom_call" | custom-call | tf_op jit(solution)/shard_map/precondition/pallas_call | solution.py:502
  140.5 2.0 %copy.5 = bf16[1,1024,320]{1,2,0:T(8,128)(2,1)} copy(bf16[1,1024,320]{1,2,0:T(8,128)(2,1)} %bitcast.9) | data formatting | bytes 1310720

commit v6 on v5

--- a/solution.py
+++ b/solution.py
@@ -553,7 +553,7 @@
             dma((2, max(n_shard, n_grp))),
         ],
         compiler_params=pltpu.CompilerParams(
-            collective_id=0, has_side_effects=True, vmem_limit_bytes=67043328
+            collective_id=0, has_side_effects=True, vmem_limit_bytes=55500000
         ),
         name="precondition",
     )(gradients[0].T, right_factor[0], left_factor[0])

time: 143 us -> 141 us (0.986)
  no operation moved by 1% of the time
where the time goes in v6:
time: 141 us; the launch traced here: 140 us
  Pallas kernels  140 us (99%)
    pallas_call x1, Pallas kernels, body(): pl.pallas_call(functools.partial(kernel, count, sizes), out_shape=jax.Sha...  140 us

profile of v6, /device:TPU:1, one launch (start us, length us, event | category | flops | bytes accessed | tf_op | source)
XLA Modules:
  0.0 140.5 jit_solution(17960171650134528114)
XLA Ops:
  0.0 139.6 %precondition.1 = bf16[320,1024]{1,0:T(8,128)(2,1)S(1)} custom-call(bf16[320,1024]{1,0:T(8,128)(2,1)} %bitcast.11, bf16[320,5120]{1,0:T(8,128)(2,1)} %bitcast.9, bf16[1024,1024]{1,0:T(8,128)(2,1)} %bitcast.10), custom_call_target="tpu_custom_call" | custom-call | tf_op jit(solution)/shard_map/precondition/pallas_call | solution.py:502
  139.7 0.8 copy.5

commit v7 on v6

--- a/solution.py
+++ b/solution.py
@@ -78,6 +78,7 @@
     final_recv,
     load_sem,
     chain_sem,
+    turn_sem,
     ar_send,
     ar_recv,
 ):
@@ -292,6 +293,17 @@
     def multiply_other(s, k):
         factor(s).wait_recv()
         first_sum[other, :] += jnp.dot(qr[s, other, :], gt[s], preferred_element_type=F32)
+
+    if n2 > 1:
+        @pl.when(g2 == 1)
+        def _():
+            pl.semaphore_wait(turn_sem, 1)
+
+    def let_go():
+        if n2 > 1:
+            @pl.when(g2 == 0)
+            def _():
+                pl.semaphore_signal(turn_sem, inc=1, device_id={"grp_2": 1 - g2}, device_id_type=MESH)
 
     loop(0, chunks, lambda c: swap(c).start())
     at_hop(0, send_factor)
@@ -312,15 +324,15 @@
 
     def hop(h):
         gather_hop(h, arrive_whole)
+        pl.when(h == 2)(let_go)
         pl.when(h == 2)(lambda: relay_home(1))
         at_hop(h, multiply_own)
         at_hop(h - 1, multiply_other)
 
     loop(2, HOPS + 1, hop)
+    pass_on(3)
     at_hop(HOPS, multiply_other)
     first[...] = first_sum[...].astype(BF16)
-
-    pass_on(3)
 
     def product(s, k):
         qrt[s] = qr[s].T
@@ -362,8 +374,6 @@
         start_last(c, k, ref)
 
     loop(0, HOPS - 2, lambda i: back_phase(HOPS - i, send_back))
-
-    pass_on(4)
 
     product(z, 0)
     kept[...] = share[0, own, :]
@@ -421,7 +431,7 @@
     total = tile[:, 0:128]
     for k in range(128, value.shape[1], 128):
         total = total + tile[:, k : k + 128]
-    mine[...] = total
+    mine[...] = jnp.sum(total, axis=0, keepdims=True)
 
     def exchange(phase, n, me, ident, slots):
         slots[me] = mine[...]
@@ -449,6 +459,7 @@
             total = total + slots[k]
         mine[...] = total
 
+    pass_on(4)
     exchange(0, n_shard, shard_me, shard_id, all_shard)
     exchange(1, n_grp, grp_me, grp_id, all_grp)
 
@@ -527,9 +538,9 @@
             pltpu.VMEM((2, nb, 2 * nb), BF16),
             pltpu.VMEM((2, nb, 2 * nb), BF16),
             pltpu.VMEM((nb, rows), F32),
-            pltpu.VMEM((8, 128), F32),
-            pltpu.VMEM((n_shard, 8, 128), F32),
-            pltpu.VMEM((n_grp, 8, 128), F32),
+            pltpu.VMEM((1, 128), F32),
+            pltpu.VMEM((n_shard, 1, 128), F32),
+            pltpu.VMEM((n_grp, 1, 128), F32),
             dma((chunks, planes)),
             dma((chunks, planes)),
             dma((chunks, planes)),
@@ -549,6 +560,7 @@
             dma((chunks,)),
             dma((planes + 3,)),
             pltpu.SemaphoreType.REGULAR((4,)),
+            pltpu.SemaphoreType.REGULAR,
             dma((2, max(n_shard, n_grp))),
             dma((2, max(n_shard, n_grp))),
         ],

time: 141 us -> 132 us (0.936)
  Pallas kernels: 140 us -> 131 us
    pallas_call x1, Pallas kernels: 140 us -> 131 us  [body(): pl.pallas_call(functools.partial(kernel, count, sizes), out_shape=jax.Sha...]
where the time goes in v7:
time: 132 us
  Pallas kernels  131 us (99%)
    pallas_call x1, Pallas kernels, body(): pl.pallas_call(functools.partial(kernel, count, sizes), out_shape=jax.Sha...  131 us

profile of v7, /device:TPU:1, one launch (start us, length us, event | category | flops | bytes accessed | tf_op | source)
XLA Modules:
  0.0 131.9 jit_solution(5513385186772725883)
XLA Ops:
  0.0 131.0 %precondition.1 = bf16[320,1024]{1,0:T(8,128)(2,1)S(1)} custom-call(bf16[320,1024]{1,0:T(8,128)(2,1)} %bitcast.11, bf16[320,5120]{1,0:T(8,128)(2,1)} %bitcast.9, bf16[1024,1024]{1,0:T(8,128)(2,1)} %bitcast.10), custom_call_target="tpu_custom_call" | custom-call | tf_op jit(solution)/shard_map/precondition/pallas_call | solution.py:513
  131.0 0.8 copy.5

commit v8 on v7

--- a/solution.py
+++ b/solution.py
@@ -206,10 +206,10 @@
         remote(held.at[c, s], held.at[c, s], back_send.at[0, 0], back_recv.at[c, s], up_z, y).wait_recv()
 
     def relayed(s):
-        return ((z <= 2) & (s == z + 4)) | ((z == 0) & (s == 5))
+        return (z == 0) & ((s == 4) | (s == 5))
 
     def relays(k):
-        return (z == 7) | ((k == 0) & ((z == 2) | (z == 3)))
+        return (z == 7) & (k >= 0)
 
     def relay_slot(s):
         return jnp.where((z == 0) & (s == 4), 1, 0)

time: 132 us -> 131 us (level)
  no operation moved by 1% of the time
where the time goes in v8:
time: 131 us
  Pallas kernels  131 us (100%)
    pallas_call x1, Pallas kernels, body(): pl.pallas_call(functools.partial(kernel, count, sizes), out_shape=jax.Sha...  131 us

profile of v8, /device:TPU:1, one launch (start us, length us, event | category | flops | bytes accessed | tf_op | source)
XLA Modules:
  0.0 131.4 jit_solution(7382624792273333671)
XLA Ops:
  0.0 130.6 %precondition.1 = bf16[320,1024]{1,0:T(8,128)(2,1)S(1)} custom-call(bf16[320,1024]{1,0:T(8,128)(2,1)} %bitcast.11, bf16[320,5120]{1,0:T(8,128)(2,1)} %bitcast.9, bf16[1024,1024]{1,0:T(8,128)(2,1)} %bitcast.10), custom_call_target="tpu_custom_call" | custom-call | tf_op jit(solution)/shard_map/precondition/pallas_call | solution.py:513
  130.6 0.8 copy.5

commit v9 on v8

--- a/solution.py
+++ b/solution.py
@@ -287,11 +287,18 @@
     def arrive_whole(c, way, s):
         down(c, s).wait_recv()
 
+    def turn(s):
+        qrt[s] = qr[s].T
+
+    def turned_early(s):
+        return (s - z < 3) | (s - z > planes - 3)
+
     def multiply_own(s, k):
         first_sum[own, :] += jnp.dot(qr[s, own, :], gt[s], preferred_element_type=F32)
 
     def multiply_other(s, k):
         factor(s).wait_recv()
+        pl.when(turned_early(s))(lambda: turn(s))
         first_sum[other, :] += jnp.dot(qr[s, other, :], gt[s], preferred_element_type=F32)
 
     if n2 > 1:
@@ -335,7 +342,7 @@
     first[...] = first_sum[...].astype(BF16)
 
     def product(s, k):
-        qrt[s] = qr[s].T
+        pl.when(jnp.logical_not(turned_early(s)))(lambda: turn(s))
         share[k] = jnp.dot(qrt[s], first[...], preferred_element_type=F32)
 
     def contribute(c, s, k, send):

time: 131 us -> 131 us (level)
  no operation moved by 1% of the time
where the time goes in v9:
time: 131 us
  Pallas kernels  131 us (100%)
    pallas_call x1, Pallas kernels, body(): pl.pallas_call(functools.partial(kernel, count, sizes), out_shape=jax.Sha...  131 us

profile of v9, /device:TPU:1, one launch (start us, length us, event | category | flops | bytes accessed | tf_op | source)
XLA Modules:
  0.0 131.4 jit_solution(7809203626029660532)
XLA Ops:
  0.0 130.6 %precondition.1 = bf16[320,1024]{1,0:T(8,128)(2,1)S(1)} custom-call(bf16[320,1024]{1,0:T(8,128)(2,1)} %bitcast.11, bf16[320,5120]{1,0:T(8,128)(2,1)} %bitcast.9, bf16[1024,1024]{1,0:T(8,128)(2,1)} %bitcast.10), custom_call_target="tpu_custom_call" | custom-call | tf_op jit(solution)/shard_map/precondition/pallas_call | solution.py:520
  130.6 0.8 copy.5
